TPU v7x, 32 devices: a whole 2x2x4 slice. The times are simulated.
32 devices in a mesh: seq: 8 (over z, y), head: 4 (over x, core).
Axes of the slice: x: 2, y: 2, z: 4, core: 2. Of those that a mesh axis runs over, the one named last changes fastest.
Arguments:
- queries: float32 [1024, 8192], P('seq', 'head'), may hold values from -48 to 48
- prefix_keys: float32 [5120, 512], P('seq', 'head'), may hold values from -5 to 5
- prefix_value_rows: float32 [5120, 512], P('seq', 'head'), may hold values from -6 to 6
- response_keys: float32 [1024, 512], P('seq', 'head'), may hold values from -6 to 6
- response_values: float32 [1024, 512], P('seq', 'head'), may hold values from -6 to 6
- out_grad: float32 [1024, 8192], P('seq', 'head'), may hold values from -6 to 6
- lengths: int32 [8], P('seq'), may hold values from 32 to 128
Outputs:
- grad_queries: float32 [1024, 8192], P(('seq', 'head'))
- grad_prefix_keys: float32 [5120, 512], P('seq', 'head')
- grad_prefix_values: float32 [5120, 512], P('seq', 'head')
- grad_resp_keys: float32 [1024, 512], P('seq', 'head')
- grad_resp_values: float32 [1024, 512], P('seq', 'head')
All inputs are finite; a program needn't handle non-finite values.
Results may differ from a plain program's by a relative error of at most 0.0003.
Values sent between devices are 32-bit elements; how exact they have to be, the bound alone decides.
A program may use at most 128 MiB of HBM per device.

v0:
```python
import functools
import math

import jax
import jax.numpy as jnp
from jax import lax
from jax.experimental import pallas as pl
from jax.experimental.pallas import tpu as pltpu
from jax.sharding import PartitionSpec as P

HEAD_SIZE = 128
WINDOW = 3
D = HEAD_SIZE
MESH = pl.DeviceIdType.MESH
F32, BF16 = jnp.float32, jnp.bfloat16
CHUNKS = 2
SUB = 128


def split(x):
    hi = x.astype(BF16)
    lo = (x - hi.astype(F32)).astype(BF16)
    return hi, lo


def dot(a, b):
    return jnp.dot(a, b, preferred_element_type=F32)


def kernel(
    n_seq, n_head,
    length_ref, q_ref, pk_ref, pv_ref, rk_ref, rv_ref, g_ref,
    gq_ref, gpk_ref, gpv_ref, grk_ref, grv_ref,
    kv1, kv2, kc, vc, kt, qt, gt, qr, gr, s_ref, dp_ref, m_ref, l_ref, d_ref,
    pcat, dcat, dk_acc, dv_acc, dqt, dqs, ry, rz,
    in_z_send, in_z_recv, in_y_send, in_y_recv,
    out_z_send, out_z_recv, out_y_send, out_y_recv,
    q_send, q_recv, q_local,
):
    rows = q_ref.shape[0]
    heads = q_ref.shape[1] // D
    pairs = heads // 2
    block = pk_ref.shape[0]
    piece = block // CHUNKS
    lead = block + rows
    off1, off2 = lead, lead + block
    factor = D ** (-0.5)
    seq = lax.axis_index("seq")
    head = lax.axis_index("head")
    even = lax.rem(seq, 2) == 0
    partner = seq + 1 - 2 * lax.rem(seq, 2)
    below = lax.rem(seq + n_seq - 2, n_seq)
    above = lax.rem(seq + 2, n_seq)

    barrier = pltpu.get_barrier_semaphore()
    for other in (partner, below, above):
        pl.semaphore_signal(barrier, inc=1, device_id=(other, head), device_id_type=MESH)
    for step in range(1, n_head):
        pl.semaphore_signal(
            barrier, inc=1, device_id=(seq, lax.rem(head + step, n_head)), device_id_type=MESH
        )
    pl.semaphore_wait(barrier, 3 + n_head - 1)

    def remote(src, dst, send, recv, to):
        return pltpu.make_async_remote_copy(
            src_ref=src, dst_ref=dst, send_sem=send, recv_sem=recv,
            device_id=to, device_id_type=MESH,
        )

    pieces = [(c, t) for c in range(CHUNKS) for t in range(2)]
    own = (pk_ref, pv_ref)

    def at(c):
        return pl.ds(c * piece, piece)

    def in_z(c, t):
        return remote(own[t].at[at(c)], kv2.at[t, at(c)], in_z_send.at[c, t], in_z_recv.at[c, t], (below, head))

    def in_y_own(c, t):
        return remote(own[t].at[at(c)], kv1.at[t, at(c)], in_y_send.at[c, t], in_y_recv.at[c, t], (partner, head))

    def in_y_pass(c, t):
        return remote(kv2.at[t, at(c)], kv1.at[t, at(c)], in_y_send.at[c, t], in_y_recv.at[c, t], (partner, head))

    for c, t in pieces:
        in_z(c, t).start()

    @pl.when(jnp.logical_not(even))
    def _():
        for c, t in pieces:
            in_y_own(c, t).start()

    length = length_ref[0]
    token = lax.broadcasted_iota(jnp.int32, (rows, 1), 0)
    live = token < length
    for h in range(heads):
        cols = pl.ds(h * D, D)
        pair, half = h // 2, h % 2
        lanes = pl.ds(half * rows, rows)
        q = q_ref[:, cols]
        g = jnp.where(live, g_ref[:, cols], 0.0)
        for x, wide, tall, scale in (
            (q, qr, qt, factor * math.log2(math.e)),
            (g, gr, gt, 1.0),
        ):
            hi, lo = split((x * scale).T)
            tall[pair, 0:D, lanes] = hi
            tall[pair, D : 2 * D, lanes] = hi
            tall[pair, 2 * D : 3 * D, lanes] = lo
            hi, lo = split(x * factor) if wide is qr else split(x)
            for copy in range(2):
                at_rows = pl.ds(copy * 2 * rows + half * rows, rows)
                wide[pair, at_rows, 0:D] = hi
                wide[pair, at_rows, D : 2 * D] = lo

    def place(keys, values, offset, size):
        for start in range(0, size, SUB):
            here = pl.ds(offset + start, SUB)
            k = keys[pl.ds(start, SUB), :]
            hi, lo = split(k)
            kc[here, 0:D] = hi
            kc[here, D : 2 * D] = lo
            kc[here, 2 * D : 3 * D] = hi
            hi, lo = split(k.T)
            kt[0:D, here] = hi
            kt[D : 2 * D, here] = lo
            hi, lo = split(values[pl.ds(start, SUB), :])
            vc[here, 0:D] = hi
            vc[here, D : 2 * D] = lo
            vc[here, 2 * D : 3 * D] = hi

    def scores(offset, size, first):
        def body(pair, carry):
            s = dot(kc[pl.ds(offset, size), :], qt[pair])
            if first:
                slot = lax.broadcasted_iota(jnp.int32, (rows, 2 * rows), 0)
                lane = lax.broadcasted_iota(jnp.int32, (rows, 2 * rows), 1)
                query = jnp.where(lane >= rows, lane - rows, lane)
                visible = (slot <= query) & (slot < length)
                s_ref[pair, pl.ds(offset, block), :] = s[:block]
                s_ref[pair, pl.ds(offset + block, rows), :] = jnp.where(visible, s[block:], -1e30)
            else:
                s_ref[pair, pl.ds(offset, size), :] = s
            dp_ref[pair, pl.ds(offset, size), :] = dot(vc[pl.ds(offset, size), :], gt[pair])
            top = None
            for start in range(0, size, SUB):
                part = jnp.max(
                    s_ref[pair, pl.ds(offset + start, SUB), :].reshape(SUB // 8, 8, 2 * rows), axis=0
                )
                top = part if top is None else jnp.maximum(top, part)
            top = jnp.max(top, axis=0, keepdims=True)
            total = jnp.zeros((8, 2 * rows), F32)
            dsum = jnp.zeros((8, 2 * rows), F32)
            for start in range(0, size, SUB):
                here = pl.ds(offset + start, SUB)
                e = jnp.exp2(s_ref[pair, here, :] - top)
                total = total + jnp.sum(e.reshape(SUB // 8, 8, 2 * rows), axis=0)
                dsum = dsum + jnp.sum((e * dp_ref[pair, here, :]).reshape(SUB // 8, 8, 2 * rows), axis=0)
            total = jnp.sum(total, axis=0, keepdims=True)
            dsum = jnp.sum(dsum, axis=0, keepdims=True)
            if first:
                m_ref[pair] = top
                l_ref[pair] = total
                d_ref[pair] = dsum
            else:
                newest = jnp.maximum(m_ref[pair], top)
                fade, add = jnp.exp2(m_ref[pair] - newest), jnp.exp2(top - newest)
                m_ref[pair] = newest
                l_ref[pair] = l_ref[pair] * fade + total * add
                d_ref[pair] = d_ref[pair] * fade + dsum * add
            return carry

        lax.fori_loop(0, pairs, body, 0)

    def grads(offset, size, first):
        keys = pl.ds(offset, size)
        dk_acc[keys, :] = jnp.zeros((size, D), F32)
        dv_acc[keys, :] = jnp.zeros((size, D), F32)

        def body(pair, carry):
            shift, mean = m_ref[pair], d_ref[pair]
            for start in range(0, size, SUB):
                here = pl.ds(offset + start, SUB)
                p = jnp.exp2(s_ref[pair, here, :] - shift)
                ds = p * (dp_ref[pair, here, :] - mean)
                to = pl.ds(start, SUB)
                hi, lo = split(p)
                pcat[to, 0 : 2 * rows] = hi
                pcat[to, 2 * rows :] = lo
                hi, lo = split(ds)
                dcat[to, 0 : 2 * rows] = hi
                dcat[to, 2 * rows :] = lo
            some = pl.ds(0, size)
            dv = dot(pcat[some, :], gr[pair])
            dv_acc[keys, :] += dv[:, :D] + dv[:, D:]
            dk = dot(dcat[some, :], qr[pair])
            dk_acc[keys, :] += dk[:, :D] + dk[:, D:]
            high = dot(kt[:, keys], dcat[some, 0 : 2 * rows])
            dq = high[:D] + high[D:] + dot(kt[0:D, keys], dcat[some, 2 * rows :])
            if first:
                dqt[pair] = dq
            else:
                dqt[pair] += dq
            return carry

        lax.fori_loop(0, pairs, body, 0)

    place(pk_ref, pv_ref, 0, block)
    place(rk_ref, rv_ref, block, rows)
    scores(0, lead, True)

    for c, t in pieces:
        in_z(c, t).wait_recv()

        @pl.when(even)
        def _():
            in_y_pass(c, t).start()

    place(kv2.at[0], kv2.at[1], off2, block)
    scores(off2, block, False)
    for c, t in pieces:
        in_y_own(c, t).wait_recv()
    place(kv1.at[0], kv1.at[1], off1, block)
    scores(off1, block, False)

    def finish(pair, carry):
        l = l_ref[pair]
        d_ref[pair] = d_ref[pair] / l
        m_ref[pair] = m_ref[pair] + jnp.log2(l)
        return carry

    lax.fori_loop(0, pairs, finish, 0)

    acc = (dk_acc, dv_acc)

    def out_y(c, t):
        return remote(
            acc[t].at[pl.ds(off1 + c * piece, piece)], ry.at[t, at(c)],
            out_y_send.at[c, t], out_y_recv.at[c, t], (partner, head),
        )

    def out_z(c, t):
        return remote(
            acc[t].at[pl.ds(off2 + c * piece, piece)], rz.at[t, at(c)],
            out_z_send.at[c, t], out_z_recv.at[c, t], (above, head),
        )

    grads(off1, block, True)
    for c, t in pieces:
        out_y(c, t).start()
    grads(off2, block, False)

    @pl.when(jnp.logical_not(even))
    def _():
        for c, t in pieces:
            out_z(c, t).start()

    grads(0, lead, False)
    grk_ref[...] = dk_acc[pl.ds(block, rows), :]
    grv_ref[...] = dv_acc[pl.ds(block, rows), :]

    for h in range(heads):
        dqs[:, pl.ds(h * D, D)] = dqt[h // 2, :, pl.ds(h % 2 * rows, rows)].T * factor

    width = heads * D
    share = rows // n_head

    def to_peer(step):
        other = lax.rem(head + step, n_head)
        return remote(
            dqs.at[pl.ds(other * share, share), :],
            gq_ref.at[:, pl.ds(pl.multiple_of(head * width, D), width)],
            q_send.at[step - 1], q_recv.at[step - 1], (seq, other),
        )

    keep = pltpu.make_async_copy(
        dqs.at[pl.ds(head * share, share), :],
        gq_ref.at[:, pl.ds(pl.multiple_of(head * width, D), width)],
        q_local,
    )
    for step in range(1, n_head):
        to_peer(step).start()
    keep.start()

    for c, t in pieces:
        out_y(c, t).wait_recv()

        @pl.when(even)
        def _():
            acc[t][pl.ds(off2 + c * piece, piece), :] += ry[t, at(c), :]
            out_z(c, t).start()

        @pl.when(jnp.logical_not(even))
        def _():
            acc[t][pl.ds(c * piece, piece), :] += ry[t, at(c), :]

    out = (gpk_ref, gpv_ref)
    for c, t in pieces:
        out_z(c, t).wait_recv()
        out[t][at(c), :] = acc[t][at(c), :] + rz[t, at(c), :]

    keep.wait()
    for step in range(1, n_head):
        to_peer(step).wait()
    for c, t in pieces:
        in_z(c, t).wait_send()
        in_y_own(c, t).wait_send()
        out_y(c, t).wait_send()
        out_z(c, t).wait_send()


def per_device(n_seq, n_head, queries, prefix_keys, prefix_value_rows, response_keys, response_values, out_grad, lengths):
    rows, width = queries.shape
    block = prefix_keys.shape[0]
    assert prefix_keys.shape[1] == D
    heads = width // D
    pairs = heads // 2
    keys = WINDOW * block + rows
    lead = block + rows
    vmem = pl.BlockSpec(memory_space=pltpu.VMEM)
    sems = pltpu.SemaphoreType.DMA((CHUNKS, 2))
    shape = jax.ShapeDtypeStruct
    return pl.pallas_call(
        functools.partial(kernel, n_seq, n_head),
        out_shape=(
            shape((rows // n_head, width * n_head), F32),
            shape((block, D), F32),
            shape((block, D), F32),
            shape((rows, D), F32),
            shape((rows, D), F32),
        ),
        in_specs=[pl.BlockSpec(memory_space=pltpu.SMEM)] + [vmem] * 6,
        out_specs=(pl.BlockSpec(memory_space=pl.ANY), vmem, vmem, vmem, vmem),
        scratch_shapes=[
            pltpu.VMEM((2, block, D), F32),
            pltpu.VMEM((2, block, D), F32),
            pltpu.VMEM((keys, 3 * D), BF16),
            pltpu.VMEM((keys, 3 * D), BF16),
            pltpu.VMEM((2 * D, keys), BF16),
            pltpu.VMEM((pairs, 3 * D, 2 * rows), BF16),
            pltpu.VMEM((pairs, 3 * D, 2 * rows), BF16),
            pltpu.VMEM((pairs, 4 * rows, 2 * D), BF16),
            pltpu.VMEM((pairs, 4 * rows, 2 * D), BF16),
            pltpu.VMEM((pairs, keys, 2 * rows), F32),
            pltpu.VMEM((pairs, keys, 2 * rows), F32),
            pltpu.VMEM((pairs, 1, 2 * rows), F32),
            pltpu.VMEM((pairs, 1, 2 * rows), F32),
            pltpu.VMEM((pairs, 1, 2 * rows), F32),
            pltpu.VMEM((lead, 4 * rows), BF16),
            pltpu.VMEM((lead, 4 * rows), BF16),
            pltpu.VMEM((keys, D), F32),
            pltpu.VMEM((keys, D), F32),
            pltpu.VMEM((pairs, D, 2 * rows), F32),
            pltpu.VMEM((rows, width), F32),
            pltpu.VMEM((2, block, D), F32),
            pltpu.VMEM((2, block, D), F32),
        ]
        + [sems] * 8
        + [pltpu.SemaphoreType.DMA((n_head - 1,))] * 2
        + [pltpu.SemaphoreType.DMA],
        compiler_params=pltpu.CompilerParams(
            collective_id=0, has_side_effects=True, vmem_limit_bytes=63 * 1024 * 1024
        ),
    )(lengths, queries, prefix_keys, prefix_value_rows, response_keys, response_values, out_grad)


def solution(mesh):
    sharded = P("seq", "head")
    return jax.shard_map(
        functools.partial(per_device, mesh.shape["seq"], mesh.shape["head"]),
        mesh=mesh,
        in_specs=(sharded,) * 6 + (P("seq"),),
        out_specs=(P(("seq", "head"), None),) + (sharded,) * 4,
        check_vma=False,
    )
```

profile of v0, /device:TPU:0, one launch (start us, length us, event | category | flops | bytes accessed | tf_op | source)
XLA Modules:
  0.0 75.9 jit_solution(10495634071805566666)
XLA Ops:
  1.3 68.9 %shard_map.110 = (f32[32,8192]{1,0:T(8,128)}, f32[640,128]{1,0:T(8,128)}, f32[640,128]{1,0:T(8,128)}, f32[128,128]{1,0:T(8,128)}, f32[128,128]{1,0:T(8,128)}) custom-call(s32[1]{0:T(128)S(6)} %copy.17.length_ref, f32[128,2048]{1,0:T(8,128)} %q_ref.1, f32[640,128]{1,0:T(8,128)} %pk_ref.1, f32[640,128]{1,0:T(8,128)} %pv_ref.1, f32[128,128]{1,0:T(8,128)} %rk_ref.1, ...), custom_call_target="tpu_custom_call" | custom-call | tf_op jit(solution)/shard_map/pallas_call | solution.py:323
  70.2 0.0 copy-start.1
  70.2 2.3 %copy.18 = f32[32,8192]{1,0:T(8,128)} copy(f32[32,8192]{1,0:T(8,128)} %get-tuple-element.10) | data formatting | bytes 2097152
  72.5 0.0 copy-done.1
  72.5 0.0 copy-start
  72.5 0.7 copy.19
  73.2 0.4 copy-done
  73.6 0.0 copy-start.3
  73.6 0.7 copy.20
  74.3 0.1 copy-done.3
  74.4 0.0 copy-start.2
  74.4 0.6 copy.21
  75.1 0.2 copy-done.2
  75.3 0.6 copy.22
Async XLA Ops:
  70.2 2.3 %copy-start.1 = (f32[640,128]{1,0:T(8,128)S(1)}, f32[640,128]{1,0:T(8,128)}, u32[]{:S(2)}) copy-start(f32[640,128]{1,0:T(8,128)} %get-tuple-element.11) | copy-start | bytes 983044
  72.5 1.1 %copy-start = (f32[640,128]{1,0:T(8,128)S(1)}, f32[640,128]{1,0:T(8,128)}, u32[]{:S(2)}) copy-start(f32[640,128]{1,0:T(8,128)} %get-tuple-element.12) | copy-start | bytes 983044
  73.6 0.9 %copy-start.3 = (f32[128,128]{1,0:T(8,128)S(1)}, f32[128,128]{1,0:T(8,128)}, u32[]{:S(2)}) copy-start(f32[128,128]{1,0:T(8,128)} %get-tuple-element.13) | copy-start | bytes 196612
  74.4 0.9 %copy-start.2 = (f32[128,128]{1,0:T(8,128)S(1)}, f32[128,128]{1,0:T(8,128)}, u32[]{:S(2)}) copy-start(f32[128,128]{1,0:T(8,128)} %get-tuple-element.14) | copy-start | bytes 196612
where the time goes:
time: 76.2 us; the launch traced here: 75.9 us
  Pallas kernels  68.9 us (90%)
  local copies, waits for them, and re-layouts  5.76 us (8%)
  between operations  1.3 us (2%)
    pallas_call x1, Pallas kernels, per_device(): pl.pallas_call(functools.partial(kernel, n_seq, n_head), out_shape=(shape...  68.9 us
    unnamed x13, local copies, waits for them, and re-layouts  5.76 us

commit v1 on v0

v1 whole, which is shorter than its diff:
```python
import functools
import math

import jax
import jax.numpy as jnp
from jax import lax
from jax.experimental import pallas as pl
from jax.experimental.pallas import tpu as pltpu
from jax.sharding import PartitionSpec as P

HEAD_SIZE = 128
WINDOW = 3
D = HEAD_SIZE
MESH = pl.DeviceIdType.MESH
F32, BF16 = jnp.float32, jnp.bfloat16
SUB = 128
UNROLL = 4


def split(x):
    hi = x.astype(BF16)
    lo = (x - hi.astype(F32)).astype(BF16)
    return hi, lo


def dot(a, b):
    return jnp.dot(a, b, preferred_element_type=F32)


def chunk_of(block):
    return (block // SUB + 1) // 2 * SUB


def kernel(
    n_seq, n_head,
    length_ref, q_hbm, pk_ref, pv_ref, rk_ref, rv_ref, g_hbm,
    gq_ref, gpk_ref, gpv_ref, grk_ref, grv_ref,
    q_ref, g_ref, kv0, kv1, kv2, kvr, kc, vc, kt, qt, gt, qr, gr, s_ref, dp_ref, m_ref, l_ref, d_ref,
    pcat, dcat, dk_acc, dv_acc, dqt, dqs, ry, rz,
    in_z_send, in_z_recv, in_y_send, in_y_recv,
    out_z_send, out_z_recv, out_y_send, out_y_recv,
    q_send, q_recv, q_local, load_sem,
):
    rows = q_hbm.shape[0]
    heads = q_hbm.shape[1] // D
    pairs = heads // 2
    block = pk_ref.shape[0]
    big = chunk_of(block)
    spans = ((0, big), (big, block - big))
    lead = block + rows
    off1, off2 = lead, lead + block
    factor = D ** (-0.5)
    seq = lax.axis_index("seq")
    head = lax.axis_index("head")
    even = lax.rem(seq, 2) == 0
    odd = jnp.logical_not(even)
    partner = seq + 1 - 2 * lax.rem(seq, 2)
    below = lax.rem(seq + n_seq - 2, n_seq)
    above = lax.rem(seq + 2, n_seq)

    barrier = pltpu.get_barrier_semaphore()
    for other in (partner, below, above):
        pl.semaphore_signal(barrier, inc=1, device_id=(other, head), device_id_type=MESH)
    for step in range(1, n_head):
        pl.semaphore_signal(
            barrier, inc=1, device_id=(seq, lax.rem(head + step, n_head)), device_id_type=MESH
        )
    loads = [
        pltpu.make_async_copy(src, dst, load_sem.at[i])
        for i, (src, dst) in enumerate(
            (
                (pk_ref, kv0.at[0]),
                (pv_ref, kv0.at[1]),
                (rk_ref, kvr.at[0]),
                (rv_ref, kvr.at[1]),
                (q_hbm, q_ref),
                (g_hbm, g_ref),
            )
        )
    ]
    for load in loads:
        load.start()
    pl.semaphore_wait(barrier, 3 + n_head - 1)

    def remote(src, dst, send, recv, to):
        return pltpu.make_async_remote_copy(
            src_ref=src, dst_ref=dst, send_sem=send, recv_sem=recv,
            device_id=to, device_id_type=MESH,
        )

    pieces = [(c, t) for c in range(2) for t in range(2)]
    own = (pk_ref, pv_ref)

    def at(c):
        return pl.ds(*spans[c])

    def in_z(c, t):
        return remote(own[t].at[at(c)], kv2.at[t, at(c)], in_z_send.at[c, t], in_z_recv.at[c, t], (below, head))

    def in_y_own(c, t):
        return remote(own[t].at[at(c)], kv1.at[t, at(c)], in_y_send.at[c, t], in_y_recv.at[c, t], (partner, head))

    def in_y_pass(c, t):
        return remote(kv2.at[t, at(c)], kv1.at[t, at(c)], in_y_send.at[c, t], in_y_recv.at[c, t], (partner, head))

    for c, t in pieces:
        in_z(c, t).start()

    @pl.when(odd)
    def _():
        for c, t in pieces:
            in_y_own(c, t).start()

    def place(keys, values, first, offset, size):
        for start in range(0, size, SUB):
            here = pl.ds(offset + start, SUB)
            k = keys[pl.ds(first + start, SUB), :]
            hi, lo = split(k)
            kc[here, 0:D] = hi
            kc[here, D : 2 * D] = lo
            kc[here, 2 * D : 3 * D] = hi
            hi, lo = split(k.T)
            kt[0:D, here] = hi
            kt[D : 2 * D, here] = lo
            hi, lo = split(values[pl.ds(first + start, SUB), :])
            vc[here, 0:D] = hi
            vc[here, D : 2 * D] = lo
            vc[here, 2 * D : 3 * D] = hi

    for load in loads[:4]:
        load.wait()
    place(kv0.at[0], kv0.at[1], 0, 0, block)
    place(kvr.at[0], kvr.at[1], 0, block, rows)
    for load in loads[4:]:
        load.wait()

    length = length_ref[0]
    token = lax.broadcasted_iota(jnp.int32, (rows, 1), 0)
    live = token < length
    for h in range(heads):
        cols = pl.ds(h * D, D)
        pair, half = h // 2, h % 2
        lanes = pl.ds(half * rows, rows)
        q = q_ref[:, cols]
        g = jnp.where(live, g_ref[:, cols], 0.0)
        for x, wide, tall, scale in (
            (q, qr, qt, factor * math.log2(math.e)),
            (g, gr, gt, 1.0),
        ):
            hi, lo = split((x * scale).T)
            tall[pair, 0:D, lanes] = hi
            tall[pair, D : 2 * D, lanes] = hi
            tall[pair, 2 * D : 3 * D, lanes] = lo
            hi, lo = split(x * factor) if wide is qr else split(x)
            for copy in range(2):
                at_rows = pl.ds(copy * 2 * rows + half * rows, rows)
                wide[pair, at_rows, 0:D] = hi
                wide[pair, at_rows, D : 2 * D] = lo

    def scores(offset, size, first):
        def products(pair):
            s = dot(kc[pl.ds(offset, size), :], qt[pair])
            if first:
                slot = lax.broadcasted_iota(jnp.int32, (rows, 2 * rows), 0)
                lane = lax.broadcasted_iota(jnp.int32, (rows, 2 * rows), 1)
                query = jnp.where(lane >= rows, lane - rows, lane)
                visible = (slot <= query) & (slot < length)
                s_ref[pair, pl.ds(offset, block), :] = s[:block]
                s_ref[pair, pl.ds(offset + block, rows), :] = jnp.where(visible, s[block:], -1e30)
            else:
                s_ref[pair, pl.ds(offset, size), :] = s
            dp_ref[pair, pl.ds(offset, size), :] = dot(vc[pl.ds(offset, size), :], gt[pair])

        def sums(pair):
            top = None
            for start in range(0, size, SUB):
                part = jnp.max(
                    s_ref[pair, pl.ds(offset + start, SUB), :].reshape(SUB // 8, 8, 2 * rows), axis=0
                )
                top = part if top is None else jnp.maximum(top, part)
            top = jnp.max(top, axis=0, keepdims=True)
            total = jnp.zeros((8, 2 * rows), F32)
            dsum = jnp.zeros((8, 2 * rows), F32)
            for start in range(0, size, SUB):
                here = pl.ds(offset + start, SUB)
                e = jnp.exp2(s_ref[pair, here, :] - top)
                total = total + jnp.sum(e.reshape(SUB // 8, 8, 2 * rows), axis=0)
                dsum = dsum + jnp.sum((e * dp_ref[pair, here, :]).reshape(SUB // 8, 8, 2 * rows), axis=0)
            total = jnp.sum(total, axis=0, keepdims=True)
            dsum = jnp.sum(dsum, axis=0, keepdims=True)
            if first:
                m_ref[pair] = top
                l_ref[pair] = total
                d_ref[pair] = dsum
            else:
                newest = jnp.maximum(m_ref[pair], top)
                fade, add = jnp.exp2(m_ref[pair] - newest), jnp.exp2(top - newest)
                m_ref[pair] = newest
                l_ref[pair] = l_ref[pair] * fade + total * add
                d_ref[pair] = d_ref[pair] * fade + dsum * add

        def body(i, carry):
            for j in range(UNROLL):
                products(i * UNROLL + j)
                if j:
                    sums(i * UNROLL + j - 1)
            sums(i * UNROLL + UNROLL - 1)
            return carry

        lax.fori_loop(0, pairs // UNROLL, body, 0)

    def grads(offset, size, first, begin=0, end=None, then=None):
        keys = pl.ds(offset, size)
        if begin == 0:
            dk_acc[keys, :] = jnp.zeros((size, D), F32)
            dv_acc[keys, :] = jnp.zeros((size, D), F32)
        some = pl.ds(0, size)

        def weights(pair, slot):
            shift, mean = m_ref[pair], d_ref[pair]
            for start in range(0, size, SUB):
                here = pl.ds(offset + start, SUB)
                p = jnp.exp2(s_ref[pair, here, :] - shift)
                ds = p * (dp_ref[pair, here, :] - mean)
                to = pl.ds(start, SUB)
                hi, lo = split(p)
                pcat[slot, to, 0 : 2 * rows] = hi
                pcat[slot, to, 2 * rows :] = lo
                hi, lo = split(ds)
                dcat[slot, to, 0 : 2 * rows] = hi
                dcat[slot, to, 2 * rows :] = lo

        def products(pair, slot):
            dv = dot(pcat[slot, some, :], gr[pair])
            dv_acc[keys, :] += dv[:, :D] + dv[:, D:]
            dk = dot(dcat[slot, some, :], qr[pair])
            dk_acc[keys, :] += dk[:, :D] + dk[:, D:]
            high = dot(kt[:, keys], dcat[slot, some, 0 : 2 * rows])
            dq = high[:D] + high[D:] + dot(kt[0:D, keys], dcat[slot, some, 2 * rows :])
            if first:
                dqt[pair] = dq
            elif then is None:
                dqt[pair] += dq
            else:
                then(pair, dqt[pair] + dq)

        def body(i, carry):
            weights(2 * i, 0)
            weights(2 * i + 1, 1)
            products(2 * i, 0)
            products(2 * i + 1, 1)
            return carry

        lax.fori_loop(begin // 2, (pairs if end is None else end) // 2, body, 0)

    scores(0, lead, True)
    for c in range(2):
        for t in range(2):
            in_z(c, t).wait_recv()

            @pl.when(even)
            def _():
                in_y_pass(c, t).start()

        place(kv2.at[0], kv2.at[1], spans[c][0], off2 + spans[c][0], spans[c][1])
        scores(off2 + spans[c][0], spans[c][1], False)
        for t in range(2):
            in_y_own(c, t).wait_recv()
        place(kv1.at[0], kv1.at[1], spans[c][0], off1 + spans[c][0], spans[c][1])
        scores(off1 + spans[c][0], spans[c][1], False)

    def finish(pair, carry):
        l = l_ref[pair]
        d_ref[pair] = d_ref[pair] / l
        m_ref[pair] = m_ref[pair] + jnp.log2(l)
        return carry

    lax.fori_loop(0, pairs, finish, 0)

    acc = (dk_acc, dv_acc)
    parts = block // SUB
    order = list(range(spans[1][0] // SUB, parts)) + list(range(spans[1][0] // SUB))
    split_at = spans[1][1] // SUB

    def out_y(i, t):
        return remote(
            acc[t].at[pl.ds(off1 + i * SUB, SUB)], ry.at[t, pl.ds(i * SUB, SUB)],
            out_y_send.at[i, t], out_y_recv.at[i, t], (partner, head),
        )

    def out_z(i, t):
        return remote(
            acc[t].at[pl.ds(off2 + i * SUB, SUB)], rz.at[t, pl.ds(i * SUB, SUB)],
            out_z_send.at[i, t], out_z_recv.at[i, t], (above, head),
        )

    def send_y(some):
        for i in some:
            for t in range(2):
                out_y(i, t).start()

    def send_z_odd(some):
        @pl.when(odd)
        def _():
            for i in some:
                for t in range(2):
                    out_z(i, t).start()

    def join(some):
        for i in some:
            for t in range(2):
                out_y(i, t).wait_recv()

            @pl.when(even)
            def _():
                for t in range(2):
                    acc[t][pl.ds(off2 + i * SUB, SUB), :] += ry[t, pl.ds(i * SUB, SUB), :]
                for t in range(2):
                    out_z(i, t).start()

    width = heads * D
    share = rows // n_head

    def to_peer(step, pair):
        other = lax.rem(head + step, n_head)
        return remote(
            dqs.at[pair, pl.ds(other * share, share), :],
            gq_ref.at[:, pl.ds(pl.multiple_of(head * width + pair * 2 * D, D), 2 * D)],
            q_send.at[step - 1, pair], q_recv.at[step - 1, pair], (seq, other),
        )

    def keep(pair):
        return pltpu.make_async_copy(
            dqs.at[pair, pl.ds(head * share, share), :],
            gq_ref.at[:, pl.ds(pl.multiple_of(head * width + pair * 2 * D, D), 2 * D)],
            q_local.at[pair],
        )

    def stage(pair, dq):
        for half in range(2):
            dqs[pair, :, half * D : (half + 1) * D] = dq[:, half * rows : (half + 1) * rows].T * factor
        for step in range(1, n_head):
            to_peer(step, pair).start()
        keep(pair).start()

    last, front = spans[1], spans[0]
    grads(off1 + last[0], last[1], True)
    send_y(order[:split_at])
    grads(off2 + last[0], last[1], False)
    send_z_odd(order[:split_at])
    grads(off1 + front[0], front[1], False)
    send_y(order[split_at:])
    join(order[:1])
    grads(off2 + front[0], front[1], False)
    send_z_odd(order[split_at:])
    join(order[1:split_at])
    middle = pairs // 4 * 2
    grads(0, lead, False, 0, middle, stage)
    join(order[split_at : split_at + 1])
    grads(0, lead, False, middle, pairs, stage)
    grk_ref[...] = dk_acc[pl.ds(block, rows), :]
    grv_ref[...] = dv_acc[pl.ds(block, rows), :]
    join(order[split_at + 1 :])

    @pl.when(odd)
    def _():
        for t in range(2):
            acc[t][pl.ds(0, block), :] += ry[t]

    out = (gpk_ref, gpv_ref)
    for i in order:
        for t in range(2):
            here = pl.ds(i * SUB, SUB)
            out_z(i, t).wait_recv()
            out[t][here, :] = acc[t][here, :] + rz[t, here, :]

    for pair in range(pairs):
        keep(pair).wait()
        for step in range(1, n_head):
            to_peer(step, pair).wait()
    for c, t in pieces:
        in_z(c, t).wait_send()
        in_y_own(c, t).wait_send()
    for i in order:
        for t in range(2):
            out_y(i, t).wait_send()
            out_z(i, t).wait_send()


def settle(*refs):
    count = len(refs) // 2
    sem = refs[-1]
    copies = [
        pltpu.make_async_copy(refs[i], refs[count + i], sem.at[i]) for i in range(count)
    ]
    for copy in copies:
        copy.start()
    for copy in copies:
        copy.wait()


def per_device(n_seq, n_head, queries, prefix_keys, prefix_value_rows, response_keys, response_values, out_grad, lengths):
    rows, width = queries.shape
    block = prefix_keys.shape[0]
    assert prefix_keys.shape[1] == D
    heads = width // D
    pairs = heads // 2
    keys = WINDOW * block + rows
    lead = block + rows
    vmem = pl.BlockSpec(memory_space=pltpu.VMEM)
    anywhere = pl.BlockSpec(memory_space=pl.ANY)
    sems = pltpu.SemaphoreType.DMA((2, 2))
    part_sems = pltpu.SemaphoreType.DMA((block // SUB, 2))
    shape = jax.ShapeDtypeStruct
    results = pl.pallas_call(
        functools.partial(kernel, n_seq, n_head),
        out_shape=(
            shape((rows // n_head, width * n_head), F32),
            shape((block, D), F32),
            shape((block, D), F32),
            shape((rows, D), F32),
            shape((rows, D), F32),
        ),
        in_specs=[pl.BlockSpec(memory_space=pltpu.SMEM)] + [anywhere] * 6,
        out_specs=(pl.BlockSpec(memory_space=pl.ANY), vmem, vmem, vmem, vmem),
        scratch_shapes=[
            pltpu.VMEM((rows, width), F32),
            pltpu.VMEM((rows, width), F32),
            pltpu.VMEM((2, block, D), F32),
            pltpu.VMEM((2, block, D), F32),
            pltpu.VMEM((2, block, D), F32),
            pltpu.VMEM((2, rows, D), F32),
            pltpu.VMEM((keys, 3 * D), BF16),
            pltpu.VMEM((keys, 3 * D), BF16),
            pltpu.VMEM((2 * D, keys), BF16),
            pltpu.VMEM((pairs, 3 * D, 2 * rows), BF16),
            pltpu.VMEM((pairs, 3 * D, 2 * rows), BF16),
            pltpu.VMEM((pairs, 4 * rows, 2 * D), BF16),
            pltpu.VMEM((pairs, 4 * rows, 2 * D), BF16),
            pltpu.VMEM((pairs, keys, 2 * rows), F32),
            pltpu.VMEM((pairs, keys, 2 * rows), F32),
            pltpu.VMEM((pairs, 1, 2 * rows), F32),
            pltpu.VMEM((pairs, 1, 2 * rows), F32),
            pltpu.VMEM((pairs, 1, 2 * rows), F32),
            pltpu.VMEM((2, lead, 4 * rows), BF16),
            pltpu.VMEM((2, lead, 4 * rows), BF16),
            pltpu.VMEM((keys, D), F32),
            pltpu.VMEM((keys, D), F32),
            pltpu.VMEM((pairs, D, 2 * rows), F32),
            pltpu.VMEM((pairs, rows, 2 * D), F32),
            pltpu.VMEM((2, block, D), F32),
            pltpu.VMEM((2, block, D), F32),
        ]
        + [sems] * 4
        + [part_sems] * 4
        + [pltpu.SemaphoreType.DMA((n_head - 1, pairs))] * 2
        + [pltpu.SemaphoreType.DMA((pairs,)), pltpu.SemaphoreType.DMA((6,))],
        compiler_params=pltpu.CompilerParams(
            collective_id=0, has_side_effects=True, vmem_limit_bytes=63 * 1024 * 1024
        ),
    )(lengths, queries, prefix_keys, prefix_value_rows, response_keys, response_values, out_grad)
    return pl.pallas_call(
        settle,
        out_shape=tuple(shape(x.shape, x.dtype) for x in results),
        in_specs=[anywhere] * len(results),
        out_specs=(anywhere,) * len(results),
        scratch_shapes=[pltpu.SemaphoreType.DMA((len(results),))],
    )(*results)


def solution(mesh):
    sharded = P("seq", "head")
    return jax.shard_map(
        functools.partial(per_device, mesh.shape["seq"], mesh.shape["head"]),
        mesh=mesh,
        in_specs=(sharded,) * 6 + (P("seq"),),
        out_specs=(P(("seq", "head"), None),) + (sharded,) * 4,
        check_vma=False,
    )
```

time: 76.2 us -> 114 us (1.50)
  Pallas kernels: 68.9 us -> 112 us
  local copies, waits for them, and re-layouts: 5.76 us -> 0 us
    pallas_call x0 -> x1, Pallas kernels: none -> 56.7 us  [per_device(): pl.pallas_call(settle, out_shape=tuple((shape(x.shape, x.dtype) for x in...]
    pallas_call x1, Pallas kernels: 68.9 us -> 55.7 us  [per_device(): pl.pallas_call(functools.partial(kernel, n_seq, n_head), out_shape=(shape...]
    unnamed x13 -> x0, local copies, waits for them, and re-layouts: 5.76 us -> none
where the time goes in v1:
time: 114 us
  Pallas kernels  112 us (98%)
  between operations  1.29 us (1%)
    pallas_call x1, Pallas kernels, per_device(): pl.pallas_call(settle, out_shape=tuple((shape(x.shape, x.dtype) for x in...  56.7 us
    pallas_call x1, Pallas kernels, per_device(): pl.pallas_call(functools.partial(kernel, n_seq, n_head), out_shape=(shape...  55.7 us

profile of v1, /device:TPU:0, one launch (start us, length us, event | category | flops | bytes accessed | tf_op | source)
XLA Modules:
  0.0 113.8 jit_solution(6977034807960513633)
XLA Ops:
  1.3 55.7 %shard_map.110 = (f32[32,8192]{1,0:T(8,128)}, f32[640,128]{1,0:T(8,128)}, f32[640,128]{1,0:T(8,128)}, f32[128,128]{1,0:T(8,128)}, f32[128,128]{1,0:T(8,128)}) custom-call(s32[1]{0:T(128)S(6)} %copy.12.length_ref, f32[128,2048]{1,0:T(8,128)} %q_hbm.1, f32[640,128]{1,0:T(8,128)} %pk_ref.1, f32[640,128]{1,0:T(8,128)} %pv_ref.1, f32[128,128]{1,0:T(8,128)} %rk_ref.1, ...), custom_call_target="tpu_custom_call" | custom-call | tf_op jit(solution)/shard_map/pallas_call | solution.py:415
  57.0 56.7 %shard_map.111 = (f32[32,8192]{1,0:T(8,128)}, f32[640,128]{1,0:T(8,128)}, f32[640,128]{1,0:T(8,128)}, f32[128,128]{1,0:T(8,128)}, f32[128,128]{1,0:T(8,128)}) custom-call(f32[32,8192]{1,0:T(8,128)} %get-tuple-element.10.refs_0_, f32[640,128]{1,0:T(8,128)} %get-tuple-element.11.refs_1_, f32[640,128]{1,0:T(8,128)} %get-tuple-element.12.refs_2_, ...), custom_call_target="tpu_custom_call" | custom-call | tf_op jit(solution)/shard_map/pallas_call | solution.py:462

commit v2 on v1

--- a/solution.py
+++ b/solution.py
@@ -388,15 +388,22 @@
 
 
 def settle(*refs):
-    count = len(refs) // 2
-    sem = refs[-1]
-    copies = [
-        pltpu.make_async_copy(refs[i], refs[count + i], sem.at[i]) for i in range(count)
+    count = (len(refs) - 2) // 3
+    load_sem, store_sem = refs[-2:]
+    held = refs[2 * count : 3 * count]
+    loads = [
+        pltpu.make_async_copy(refs[i], held[i], load_sem.at[i]) for i in range(count)
     ]
-    for copy in copies:
-        copy.start()
-    for copy in copies:
-        copy.wait()
+    stores = [
+        pltpu.make_async_copy(held[i], refs[count + i], store_sem.at[i]) for i in range(count)
+    ]
+    for load in loads:
+        load.start()
+    for load, store in zip(loads, stores):
+        load.wait()
+        store.start()
+    for store in stores:
+        store.wait()
 
 
 def per_device(n_seq, n_head, queries, prefix_keys, prefix_value_rows, response_keys, response_values, out_grad, lengths):
@@ -464,7 +471,8 @@
         out_shape=tuple(shape(x.shape, x.dtype) for x in results),
         in_specs=[anywhere] * len(results),
         out_specs=(anywhere,) * len(results),
-        scratch_shapes=[pltpu.SemaphoreType.DMA((len(results),))],
+        scratch_shapes=[pltpu.VMEM(x.shape, x.dtype) for x in results]
+        + [pltpu.SemaphoreType.DMA((len(results),))] * 2,
     )(*results)
 
 

time: 114 us -> 59.7 us (0.52)
  Pallas kernels: 112 us -> 58.3 us
    pallas_call x1, Pallas kernels: 56.7 us -> 2.52 us  [per_device(): pl.pallas_call(settle, out_shape=tuple((shape(x.shape, x.dtype) for x in...]
where the time goes in v2:
time: 59.7 us; the launch traced here: 59.5 us
  Pallas kernels  58.3 us (98%)
  between operations  1.29 us (2%)
    pallas_call x1, Pallas kernels, per_device(): pl.pallas_call(functools.partial(kernel, n_seq, n_head), out_shape=(shape...  55.7 us
    pallas_call x1, Pallas kernels, per_device(): pl.pallas_call(settle, out_shape=tuple((shape(x.shape, x.dtype) for x in...  2.52 us

profile of v2, /device:TPU:0, one launch (start us, length us, event | category | flops | bytes accessed | tf_op | source)
XLA Modules:
  0.0 59.5 jit_solution(12312639916899991267)
XLA Ops:
  1.3 55.7 %shard_map.110 = (f32[32,8192]{1,0:T(8,128)}, f32[640,128]{1,0:T(8,128)}, f32[640,128]{1,0:T(8,128)}, f32[128,128]{1,0:T(8,128)}, f32[128,128]{1,0:T(8,128)}) custom-call(s32[1]{0:T(128)S(6)} %copy.12.length_ref, f32[128,2048]{1,0:T(8,128)} %q_hbm.1, f32[640,128]{1,0:T(8,128)} %pk_ref.1, f32[640,128]{1,0:T(8,128)} %pv_ref.1, f32[128,128]{1,0:T(8,128)} %rk_ref.1, ...), custom_call_target="tpu_custom_call" | custom-call | tf_op jit(solution)/shard_map/pallas_call | solution.py:422
  57.0 2.5 %shard_map.111 = (f32[32,8192]{1,0:T(8,128)}, f32[640,128]{1,0:T(8,128)}, f32[640,128]{1,0:T(8,128)}, f32[128,128]{1,0:T(8,128)}, f32[128,128]{1,0:T(8,128)}) custom-call(f32[32,8192]{1,0:T(8,128)} %get-tuple-element.10.refs_0_, f32[640,128]{1,0:T(8,128)} %get-tuple-element.11.refs_1_, f32[640,128]{1,0:T(8,128)} %get-tuple-element.12.refs_2_, ...), custom_call_target="tpu_custom_call" | custom-call | tf_op jit(solution)/shard_map/pallas_call | solution.py:469
